TPU v7x, 32 devices: a whole 2x2x4 slice. The times are simulated.
32 devices in a mesh: rows: 4 (over z), tp: 4 (over y, x), unit: 2 (over core).
Axes of the slice: x: 2, y: 2, z: 4, core: 2. Of those that a mesh axis runs over, the one named last changes fastest.
Arguments:
- w_query: bfloat16 [5120, 4096], P(('unit', 'rows'), 'tp'), parts along dimension 0, may hold values from -0.125 to 0.125
- low_query: bfloat16 [5120, 64], P(('unit', 'rows')), parts along dimension 0, may hold values from -0.125 to 0.125
- high_query: bfloat16 [128, 4096], P('unit', 'tp'), parts along dimension 0, may hold values from -0.75 to 0.75
- w_key: bfloat16 [5120, 1024], P(('unit', 'rows'), 'tp'), parts along dimension 0, may hold values from -0.125 to 0.125
- low_key: bfloat16 [5120, 64], P(('unit', 'rows')), parts along dimension 0, may hold values from -0.125 to 0.125
- high_key: bfloat16 [128, 1024], P('unit', 'tp'), parts along dimension 0, may hold values from -0.75 to 0.75
- w_value: bfloat16 [5120, 1024], P(('unit', 'rows'), 'tp'), parts along dimension 0, may hold values from -0.125 to 0.125
- low_value: bfloat16 [5120, 64], P(('unit', 'rows')), parts along dimension 0, may hold values from -0.125 to 0.125
- high_value: bfloat16 [128, 1024], P('unit', 'tp'), parts along dimension 0, may hold values from -0.75 to 0.75
- w_mixed: bfloat16 [8192, 2560], P(('unit', 'tp'), 'rows'), parts along dimension 0, may hold values from -0.09375 to 0.09375
- low_mixed: bfloat16 [8192, 64], P(('unit', 'tp')), parts along dimension 0, may hold values from -0.09375 to 0.09375
- high_mixed: bfloat16 [128, 2560], P('unit', 'rows'), parts along dimension 0, may hold values from -0.75 to 0.75
- norm_train: float32 [5120], P(('unit', 'rows', 'tp')), parts along dimension 0, may hold values from 0.25 to 1.75
- norm_step: float32 [5120], P(('unit', 'rows', 'tp')), parts along dimension 0, may hold values from -0.3 to 0.3
Outputs:
- final_query: bfloat16 [5120, 4096], P('unit', 'tp'), parts along dimension 0
- final_key: bfloat16 [5120, 1024], P('unit', 'tp'), parts along dimension 0
- final_value: bfloat16 [5120, 1024], P('unit', 'tp'), parts along dimension 0
- final_mixed: bfloat16 [8192, 2560], P(('unit', 'tp')), parts along dimension 0
- serve_norm: bfloat16 [5120], P('unit'), parts along dimension 0
There are 2 independent parts, one for each index of `unit`. A program takes and returns all parts, laid end to end along the dimension named above; each array names one. Nothing has to cross between parts.
All inputs are finite; a program needn't handle non-finite values.
Results may differ from a plain program's by a relative error of at most 0.001.
Values may be sent and summed in bfloat16 or wider, within the bound.
A program may use at most 128 MiB of HBM per device.

v0:
```python
import functools

import jax
import jax.numpy as jnp
from jax import lax
from jax.experimental import pallas as pl
from jax.experimental.pallas import tpu as pltpu
from jax.sharding import PartitionSpec as P

MESH = pl.DeviceIdType.MESH
mix_rate = 0.5
chunk_bytes = 700 * 1024
first_bytes = 200 * 1024
order = (1, 0, 3, 2)


def pieces_of(rows, columns, most):
    count = 1
    while rows * columns * 2 > count * most and rows % (count * 32) == 0:
        count *= 2
    return count


def block_of(size, options):
    for option in options:
        if size % option == 0:
            return option
    return size


def kernel(n, tps, stacked, pieces, *refs):
    kinds = len(pieces)
    w, low, high = refs[:kinds], refs[kinds : 2 * kinds], refs[2 * kinds : 3 * kinds]
    norm_train, norm_step = refs[3 * kinds : 3 * kinds + 2]
    refs = refs[3 * kinds + 2 :]
    out, norm_out = refs[:kinds], refs[kinds]
    refs = refs[kinds + 1 :]
    w_own, low_own, high_own = refs[:kinds], refs[kinds : 2 * kinds], refs[2 * kinds : 3 * kinds]
    low_rows = refs[3 * kinds : 4 * kinds]
    refs = refs[4 * kinds :]
    norm_own, norm_all, norm_sem, load_sem, side_sem, send_sem, recv_sem, pass_send, pass_recv, norm_send, norm_recv, cross_send, cross_recv = refs

    z, t = lax.axis_index("rows"), lax.axis_index("tp")
    chunks = [(k, p) for k in order for p in range(pieces[k])]
    has_up, has_down = z < n - 1, z > 0

    def rows_of(k, p):
        size = w[k].shape[0] // pieces[k]
        return p * size, size

    def load(i):
        k, p = chunks[i]
        start, size = rows_of(k, p)
        return pltpu.make_async_copy(
            w[k].at[pl.ds(start, size)], w_own[k].at[pl.ds(start, size)], load_sem.at[i]
        )

    def side(k):
        return (
            pltpu.make_async_copy(low[k], low_own[k], side_sem.at[0, k]),
            pltpu.make_async_copy(high[k], high_own[k], side_sem.at[1, k]),
        )

    def load_kind(kind):
        for copy in side(kind):
            copy.start()
        for i, (k, p) in enumerate(chunks):
            if k == kind:
                load(i).start()

    load_kind(order[0])

    barrier = pltpu.get_barrier_semaphore()

    @pl.when(has_up)
    def _():
        pl.semaphore_signal(barrier, inc=1, device_id={"rows": z + 1}, device_id_type=MESH)

    @pl.when(has_down)
    def _():
        pl.semaphore_signal(barrier, inc=1, device_id={"rows": z - 1}, device_id_type=MESH)

    for step in range(1, tps):
        pl.semaphore_signal(barrier, inc=1, device_id={"tp": lax.rem(t + step, tps)}, device_id_type=MESH)

    for kind in order[1:]:
        load_kind(kind)

    norm_loads = [
        pltpu.make_async_copy(source, norm_own.at[j], norm_sem.at[j])
        for j, source in enumerate((norm_train, norm_step))
    ]
    for copy in norm_loads:
        copy.start()

    def region(k, p, origin):
        start, size = (0, w[k].shape[0]) if p is None else rows_of(k, p)
        columns = w[k].shape[1]
        if stacked[k]:
            return out[k].at[origin, pl.ds(start, size)]
        if out[k].shape[1] == columns:
            rows = w[k].shape[0]
            return out[k].at[pl.ds(pl.multiple_of(origin * rows + start, 16), size)]
        return out[k].at[pl.ds(start, size), pl.ds(pl.multiple_of(origin * columns, 128), columns)]

    def hop(place, send, recv, direction):
        return pltpu.make_async_remote_copy(
            src_ref=place,
            dst_ref=place,
            send_sem=send,
            recv_sem=recv,
            device_id={"rows": z + 1 - 2 * direction},
            device_id_type=MESH,
        )

    def chunk_hop(i, origin, direction):
        k, p = chunks[i]
        return hop(region(k, p, origin), send_sem.at[direction, i], recv_sem.at[direction, i], direction)

    def whole_hop(k, origin, direction):
        return hop(
            region(k, None, origin),
            pass_send.at[direction, origin, k],
            pass_recv.at[direction, origin, k],
            direction,
        )

    def norm_hop(origin, direction):
        return pltpu.make_async_remote_copy(
            src_ref=norm_all.at[origin, t],
            dst_ref=norm_all.at[origin, t],
            send_sem=norm_send.at[direction, origin],
            recv_sem=norm_recv.at[direction, origin],
            device_id={"rows": z + 1 - 2 * direction},
            device_id_type=MESH,
        )

    def cross(step, column):
        return pltpu.make_async_remote_copy(
            src_ref=norm_all.at[:, column],
            dst_ref=norm_all.at[:, column],
            send_sem=cross_send.at[step],
            recv_sem=cross_recv.at[step],
            device_id={"tp": lax.rem(t + step, tps)},
            device_id_type=MESH,
        )

    def send_both(make):
        @pl.when(has_up)
        def _():
            make(0).start()

        @pl.when(has_down)
        def _():
            make(1).start()

    def merge(i):
        k, p = chunks[i]
        start, size = rows_of(k, p)
        columns = w[k].shape[1]
        high_block = block_of(size, (160, 128, 64, 32, 16))
        wide_block = block_of(columns, (256, 128))
        wides = columns // wide_block
        place = region(k, p, z)

        def body(b, _):
            if size == high_block:
                r, c = 0, b
            else:
                r, c = b // wides, b % wides
            r = r * high_block
            c = 0 if wides == 1 else pl.multiple_of(c * wide_block, wide_block)
            mine = pl.ds(start + r, high_block)
            wide = pl.ds(c, wide_block)
            result = w_own[k][mine, wide].astype(jnp.float32) + mix_rate * jnp.dot(
                low_rows[k][mine, :], high_own[k][:, wide], preferred_element_type=jnp.float32
            )
            place[pl.ds(r, high_block), wide] = result.astype(jnp.bfloat16)
            return 0

        lax.fori_loop(0, (size // high_block) * wides, body, 0)

    for i, (k, p) in enumerate(chunks):
        if p == 0:
            for copy in side(k):
                copy.wait()
            low_rows[k][...] = low_own[k][...].astype(jnp.float32).T.astype(jnp.bfloat16)
        load(i).wait()
        merge(i)
        if i == 1:
            partners = has_up.astype(jnp.int32) + has_down.astype(jnp.int32) + tps - 1
            pl.semaphore_wait(barrier, partners)
        if i > 0:
            send_both(functools.partial(chunk_hop, i - 1, z))
        if i == 1:
            for copy in norm_loads:
                copy.wait()
            norm_all[z, t] = (norm_own[0] + norm_own[1]).astype(jnp.bfloat16).astype(jnp.float32)
        if i == min(2, len(chunks) - 1):
            send_both(functools.partial(norm_hop, z))
    send_both(functools.partial(chunk_hop, len(chunks) - 1, z))

    def arrival(arrived, onward, d):
        below, above = z - d, z + d

        @pl.when(below >= 0)
        def _():
            for make in arrived:
                make(below, 0).wait_recv()

            @pl.when(has_up)
            def _():
                onward(below, 0).start()

        @pl.when(above < n)
        def _():
            for make in arrived:
                make(above, 1).wait_recv()

            @pl.when(has_down)
            def _():
                onward(above, 1).start()

    def distance(d, _, near=False):
        arrival([norm_hop], norm_hop, d)

        @pl.when(d == n - 1)
        def _():
            for step in range(1, tps):
                cross(step, t).start()

        for k in order:
            onward = functools.partial(whole_hop, k)
            arrived = [onward]
            if near:
                arrived = [functools.partial(chunk_hop, i) for i, c in enumerate(chunks) if c[0] == k]
            if k == order[-1]:

                @pl.when(d == n - 1)
                def _():
                    all_norms()

            arrival(arrived, onward, d)
        return 0

    def all_norms():
        for step in range(1, tps):
            cross(step, lax.rem(t + tps - step, tps)).wait_recv()
        line = jnp.concatenate([norm_all[a, b] for a in range(n) for b in range(tps)], axis=1)
        width = norm_out.shape[1]
        norm_out[...] = jnp.concatenate(
            [line[:, a * width : (a + 1) * width] for a in range(norm_out.shape[0])], axis=0
        ).astype(jnp.bfloat16)

    distance(jnp.int32(1), 0, near=True)
    lax.fori_loop(2, n, distance, 0)

    for direction, flag in ((0, has_up), (1, has_down)):

        @pl.when(flag)
        def _():
            for i in range(len(chunks)):
                chunk_hop(i, z, direction).wait_send()
            norm_hop(z, direction).wait_send()

    def drain(origin, _):
        for direction, flag in ((0, has_up & (origin < z)), (1, has_down & (origin > z))):

            @pl.when(flag)
            def _():
                for k in range(kinds):
                    whole_hop(k, origin, direction).wait_send()
                norm_hop(origin, direction).wait_send()

        return 0

    lax.fori_loop(0, n, drain, 0)
    for step in range(1, tps):
        cross(step, t).wait_send()


def put(parts, *refs):
    kinds = len(parts)
    src, dst, sem = refs[:kinds], refs[kinds : 2 * kinds], refs[2 * kinds]
    copies = []
    for k in range(kinds):
        size = src[k].shape[0] // parts[k]
        for p in range(parts[k]):
            rows = pl.ds(p * size, size)
            copies.append(pltpu.make_async_copy(src[k].at[rows], dst[k].at[rows], sem.at[len(copies)]))
    for copy in copies:
        copy.start()
    for copy in copies:
        copy.wait()


def place(arrays):
    parts = [2 if x.shape[0] % 128 == 0 else 1 for x in arrays]
    return pl.pallas_call(
        functools.partial(put, parts),
        out_shape=[jax.ShapeDtypeStruct(x.shape, x.dtype) for x in arrays],
        in_specs=[pl.BlockSpec(memory_space=pltpu.VMEM)] * len(arrays),
        out_specs=[pl.BlockSpec(memory_space=pltpu.HBM)] * len(arrays),
        scratch_shapes=[pltpu.SemaphoreType.DMA((sum(parts),))],
        compiler_params=pltpu.CompilerParams(vmem_limit_bytes=24 * 1024 * 1024),
        name="place",
    )(*arrays)


def shards(n, tps, *args):
    w, low, high = args[0:12:3], [x.T for x in args[1:12:3]], args[2:12:3]
    norm_train, norm_step = args[12].reshape(1, -1), args[13].reshape(1, -1)
    kinds = len(w)
    by_column = [False] * (kinds - 1) + [True]
    stacked = [by_column[k] and w[k].shape[1] % 128 != 0 for k in range(kinds)]
    most = {order[0]: first_bytes, order[1]: chunk_bytes}
    pieces = [pieces_of(*w[k].shape, most.get(k, w[k].size * 2)) for k in range(kinds)]
    count = sum(pieces)
    shapes = []
    for k in range(kinds):
        rows, columns = w[k].shape
        if stacked[k]:
            shapes.append((n, rows, columns))
        elif by_column[k]:
            shapes.append((rows, n * columns))
        else:
            shapes.append((n * rows, columns))
    share = norm_train.shape[1]
    total = n * tps * share
    width = 128 if total % 128 == 0 else total
    vmem, hbm = pl.BlockSpec(memory_space=pltpu.VMEM), pl.BlockSpec(memory_space=pltpu.HBM)
    dma = pltpu.SemaphoreType.DMA
    operands = (*w, *low, *high, norm_train, norm_step)
    results = pl.pallas_call(
        functools.partial(kernel, n, tps, stacked, pieces),
        out_shape=[pltpu.VMEM(s, jnp.bfloat16) for s in shapes]
        + [pltpu.VMEM((total // width, width), jnp.bfloat16)],
        in_specs=[hbm] * (3 * kinds + 2),
        out_specs=[vmem] * (kinds + 1),
        scratch_shapes=[pltpu.VMEM(x.shape, x.dtype) for x in (*w, *low, *high)]
        + [pltpu.VMEM(x.shape[::-1], x.dtype) for x in low]
        + [
            pltpu.VMEM((2, 1, share), jnp.float32),
            pltpu.VMEM((n, tps, 1, share), jnp.float32),
            dma((2,)),
            dma((count,)),
            dma((2, kinds)),
            dma((2, count)),
            dma((2, count)),
            dma((2, n, kinds)),
            dma((2, n, kinds)),
            dma((2, n)),
            dma((2, n)),
            dma((tps,)),
            dma((tps,)),
        ],
        compiler_params=pltpu.CompilerParams(
            collective_id=0, has_side_effects=True, vmem_limit_bytes=24 * 1024 * 1024
        ),
        name="merge_and_gather",
    )(*[pltpu.with_memory_space_constraint(x, pltpu.HBM) for x in operands])
    results = place(results)
    finals = []
    for k in range(kinds):
        full = results[k]
        if stacked[k]:
            full = full.transpose(1, 0, 2).reshape(full.shape[1], -1)
        finals.append(full)
    return (*finals, results[kinds].reshape(-1))


def solution(mesh):
    return jax.shard_map(
        functools.partial(shards, mesh.shape["rows"], mesh.shape["tp"]),
        mesh=mesh,
        in_specs=(
            P(("unit", "rows"), "tp"),
            P(("unit", "rows"), None),
            P("unit", "tp"),
            P(("unit", "rows"), "tp"),
            P(("unit", "rows"), None),
            P("unit", "tp"),
            P(("unit", "rows"), "tp"),
            P(("unit", "rows"), None),
            P("unit", "tp"),
            P(("unit", "tp"), "rows"),
            P(("unit", "tp"), None),
            P("unit", "rows"),
            P(("unit", "rows", "tp")),
            P(("unit", "rows", "tp")),
        ),
        out_specs=(
            P("unit", "tp"),
            P("unit", "tp"),
            P("unit", "tp"),
            P(("unit", "tp"), None),
            P("unit"),
        ),
        check_vma=False,
    )
```

profile of v0, /device:TPU:1, one launch (start us, length us, event | category | flops | bytes accessed | tf_op | source)
XLA Modules:
  0.0 221.8 jit_solution(4210453455522618952)
XLA Ops:
  0.6 216.3 %merge_and_gather.1 = (bf16[2560,1024]{1,0:T(8,128)(2,1)S(1)}, bf16[2560,256]{1,0:T(8,128)(2,1)S(1)}, bf16[2560,256]{1,0:T(8,128)(2,1)S(1)}, bf16[1024,2560]{1,0:T(8,128)(2,1)S(1)}, bf16[20,128]{1,0:T(8,128)(2,1)S(1)}) custom-call(bf16[640,1024]{1,0:T(8,128)(2,1)} %refs_0_.1, bf16[640,256]{1,0:T(8,128)(2,1)} %refs_1_.1, bf16[640,256]{1,0:T(8,128)(2,1)} %refs_2_.1, ...), custom_call_target="tpu_custom_call" | custom-call | tf_op jit(solution)/shard_map/merge_and_gather/pallas_call | solution.py:334
  217.0 4.9 %place.1 = (bf16[2560,1024]{1,0:T(8,128)(2,1)}, bf16[2560,256]{1,0:T(8,128)(2,1)}, bf16[2560,256]{1,0:T(8,128)(2,1)}, bf16[1024,2560]{1,0:T(8,128)(2,1)}, bf16[20,128]{1,0:T(8,128)(2,1)}) custom-call(bf16[2560,1024]{1,0:T(8,128)(2,1)S(1)} %get-tuple-element.15.refs_0_, bf16[2560,256]{1,0:T(8,128)(2,1)S(1)} %get-tuple-element.16.refs_1_, ...), custom_call_target="tpu_custom_call" | custom-call | tf_op jit(solution)/shard_map/place/pallas_call | solution.py:299
where the time goes:
time: 224 us; the launch traced here: 222 us
  Pallas kernels  221 us (99%)
    pallas_call x1, Pallas kernels, shards(): pl.pallas_call(functools.partial(kernel, n, tps, stacked, pieces), out_sh...  216 us
    pallas_call x1, Pallas kernels, place(): pl.pallas_call(functools.partial(put, parts), out_shape=[jax.ShapeDtypeSt...  4.88 us

commit v1 on v0

--- a/solution.py
+++ b/solution.py
@@ -9,16 +9,27 @@
 
 MESH = pl.DeviceIdType.MESH
 mix_rate = 0.5
-chunk_bytes = 700 * 1024
-first_bytes = 200 * 1024
 order = (1, 0, 3, 2)
-
-
-def pieces_of(rows, columns, most):
-    count = 1
-    while rows * columns * 2 > count * most and rows % (count * 32) == 0:
-        count *= 2
-    return count
+late_kind = order[-1]
+
+
+def pieces_of(rows, firsts):
+    sizes = [size for size in firsts if sum(firsts) < rows]
+    left = rows - sum(sizes)
+    return [*sizes, left] if left % 16 == 0 or not sizes else [rows]
+
+
+def rounds_of(tps, t):
+    if tps & (tps - 1):
+        return [[(lax.rem(t + step, tps), t, lax.rem(t + tps - step, tps), 1) for step in range(1, tps)]]
+    rounds, size = [], 1
+    while size < tps:
+        side = lax.rem(t // size, 2)
+        base = (t // size) * size
+        across = size - 2 * size * side
+        rounds.append([(t + across, base, base + across, size)])
+        size *= 2
+    return rounds
 
 
 def block_of(size, options):
@@ -28,7 +39,7 @@
     return size
 
 
-def kernel(n, tps, stacked, pieces, *refs):
+def kernel(n, tps, units, stacked, pieces, *refs):
     kinds = len(pieces)
     w, low, high = refs[:kinds], refs[kinds : 2 * kinds], refs[2 * kinds : 3 * kinds]
     norm_train, norm_step = refs[3 * kinds : 3 * kinds + 2]
@@ -41,12 +52,23 @@
     norm_own, norm_all, norm_sem, load_sem, side_sem, send_sem, recv_sem, pass_send, pass_recv, norm_send, norm_recv, cross_send, cross_recv = refs
 
     z, t = lax.axis_index("rows"), lax.axis_index("tp")
-    chunks = [(k, p) for k in order for p in range(pieces[k])]
+    late = lax.axis_index("unit") == units - 1
+    rounds = rounds_of(tps, t)
+    chunks = [(k, p) for k in order for p in range(len(pieces[k]))]
     has_up, has_down = z < n - 1, z > 0
+    held_up, held_down = late & (z == n - 2), late & (z == 1)
+    missing_up, missing_down = late & (z == n - 1), late & (z == 0)
+
+    def sends(k, direction):
+        has, held = ((has_up, held_up), (has_down, held_down))[direction]
+        return has & ~held if k == late_kind else has
+
+    def comes(k, d, direction):
+        has, missing = ((z - d >= 0, missing_up), (z + d < n, missing_down))[direction]
+        return has & ~missing if k == late_kind else has
 
     def rows_of(k, p):
-        size = w[k].shape[0] // pieces[k]
-        return p * size, size
+        return sum(pieces[k][:p]), pieces[k][p]
 
     def load(i):
         k, p = chunks[i]
@@ -80,8 +102,8 @@
     def _():
         pl.semaphore_signal(barrier, inc=1, device_id={"rows": z - 1}, device_id_type=MESH)
 
-    for step in range(1, tps):
-        pl.semaphore_signal(barrier, inc=1, device_id={"tp": lax.rem(t + step, tps)}, device_id_type=MESH)
+    for partner in [exchange[0] for exchanges in rounds for exchange in exchanges]:
+        pl.semaphore_signal(barrier, inc=1, device_id={"tp": partner}, device_id_type=MESH)
 
     for kind in order[1:]:
         load_kind(kind)
@@ -135,24 +157,32 @@
             device_id_type=MESH,
         )
 
-    def cross(step, column):
+    def cross(r, j, coming=False):
+        partner, base, theirs, size = rounds[r][j]
+        place = norm_all.at[:, pl.ds(theirs if coming else base, size)]
         return pltpu.make_async_remote_copy(
-            src_ref=norm_all.at[:, column],
-            dst_ref=norm_all.at[:, column],
-            send_sem=cross_send.at[step],
-            recv_sem=cross_recv.at[step],
-            device_id={"tp": lax.rem(t + step, tps)},
+            src_ref=place,
+            dst_ref=place,
+            send_sem=cross_send.at[r, j],
+            recv_sem=cross_recv.at[r, j],
+            device_id={"tp": partner},
             device_id_type=MESH,
         )
 
-    def send_both(make):
-        @pl.when(has_up)
-        def _():
-            make(0).start()
-
-        @pl.when(has_down)
-        def _():
-            make(1).start()
+    def cross_start(r):
+        for j in range(len(rounds[r])):
+            cross(r, j).start()
+
+    def cross_wait(r):
+        for j in range(len(rounds[r])):
+            cross(r, j, coming=True).wait_recv()
+
+    def send_both(make, k=None):
+        for direction in range(2):
+
+            @pl.when(sends(k, direction))
+            def _():
+                make(direction).start()
 
     def merge(i):
         k, p = chunks[i]
@@ -188,48 +218,38 @@
         load(i).wait()
         merge(i)
         if i == 1:
-            partners = has_up.astype(jnp.int32) + has_down.astype(jnp.int32) + tps - 1
+            partners = has_up.astype(jnp.int32) + has_down.astype(jnp.int32) + sum(map(len, rounds))
             pl.semaphore_wait(barrier, partners)
         if i > 0:
-            send_both(functools.partial(chunk_hop, i - 1, z))
-        if i == 1:
+            send_both(functools.partial(chunk_hop, i - 1, z), chunks[i - 1][0])
+        if i == min(3, len(chunks) - 2):
             for copy in norm_loads:
                 copy.wait()
             norm_all[z, t] = (norm_own[0] + norm_own[1]).astype(jnp.bfloat16).astype(jnp.float32)
-        if i == min(2, len(chunks) - 1):
+        if i == min(4, len(chunks) - 1):
             send_both(functools.partial(norm_hop, z))
-    send_both(functools.partial(chunk_hop, len(chunks) - 1, z))
-
-    def arrival(arrived, onward, d):
-        below, above = z - d, z + d
-
-        @pl.when(below >= 0)
-        def _():
-            for make in arrived:
-                make(below, 0).wait_recv()
-
-            @pl.when(has_up)
+    send_both(functools.partial(chunk_hop, len(chunks) - 1, z), chunks[-1][0])
+
+    def arrival(arrived, onward, d, k=None):
+        for direction, origin in ((0, z - d), (1, z + d)):
+
+            @pl.when(comes(k, d, direction))
             def _():
-                onward(below, 0).start()
-
-        @pl.when(above < n)
-        def _():
-            for make in arrived:
-                make(above, 1).wait_recv()
-
-            @pl.when(has_down)
-            def _():
-                onward(above, 1).start()
+                for make in arrived:
+                    make(origin, direction).wait_recv()
+
+                @pl.when(sends(k, direction))
+                def _():
+                    onward(origin, direction).start()
 
     def distance(d, _, near=False):
         arrival([norm_hop], norm_hop, d)
 
         @pl.when(d == n - 1)
         def _():
-            for step in range(1, tps):
-                cross(step, t).start()
-
-        for k in order:
+            cross_start(0)
+
+        for j, k in enumerate(order):
             onward = functools.partial(whole_hop, k)
             arrived = [onward]
             if near:
@@ -240,12 +260,14 @@
                 def _():
                     all_norms()
 
-            arrival(arrived, onward, d)
+            arrival(arrived, onward, d, k)
         return 0
 
     def all_norms():
-        for step in range(1, tps):
-            cross(step, lax.rem(t + tps - step, tps)).wait_recv()
+        for r in range(len(rounds)):
+            if r > 0:
+                cross_start(r)
+            cross_wait(r)
         line = jnp.concatenate([norm_all[a, b] for a in range(n) for b in range(tps)], axis=1)
         width = norm_out.shape[1]
         norm_out[...] = jnp.concatenate(
@@ -255,67 +277,195 @@
     distance(jnp.int32(1), 0, near=True)
     lax.fori_loop(2, n, distance, 0)
 
-    for direction, flag in ((0, has_up), (1, has_down)):
-
-        @pl.when(flag)
-        def _():
-            for i in range(len(chunks)):
+    for direction in range(2):
+        for i in range(len(chunks)):
+
+            @pl.when(sends(chunks[i][0], direction))
+            def _():
                 chunk_hop(i, z, direction).wait_send()
+
+        @pl.when(sends(None, direction))
+        def _():
             norm_hop(z, direction).wait_send()
 
     def drain(origin, _):
-        for direction, flag in ((0, has_up & (origin < z)), (1, has_down & (origin > z))):
-
-            @pl.when(flag)
+        for direction, passed in ((0, origin < z), (1, origin > z)):
+            for k in range(kinds):
+
+                @pl.when(sends(k, direction) & passed)
+                def _():
+                    whole_hop(k, origin, direction).wait_send()
+
+            @pl.when(sends(None, direction) & passed)
             def _():
-                for k in range(kinds):
-                    whole_hop(k, origin, direction).wait_send()
                 norm_hop(origin, direction).wait_send()
 
         return 0
 
     lax.fori_loop(0, n, drain, 0)
-    for step in range(1, tps):
-        cross(step, t).wait_send()
-
-
-def put(parts, *refs):
+    for r in range(len(rounds)):
+        for j in range(len(rounds[r])):
+            cross(r, j).wait_send()
+
+
+def ends(n, units):
+    z, late = lax.axis_index("rows"), lax.axis_index("unit") == units - 1
+    return late & (z == 0), late & (z == n - 1)
+
+
+def put(n, units, parts, *refs):
     kinds = len(parts)
-    src, dst, sem = refs[:kinds], refs[kinds : 2 * kinds], refs[2 * kinds]
-    copies = []
+    src, dst, sem = refs[:kinds], refs[kinds : 2 * kinds], refs[-1]
+    bottom, top = ends(n, units)
+    copies, kept = [], []
     for k in range(kinds):
         size = src[k].shape[0] // parts[k]
         for p in range(parts[k]):
             rows = pl.ds(p * size, size)
-            copies.append(pltpu.make_async_copy(src[k].at[rows], dst[k].at[rows], sem.at[len(copies)]))
+            copy = pltpu.make_async_copy(src[k].at[rows], dst[k].at[rows], sem.at[len(copies) + len(kept)])
+            (kept if k == late_kind else copies).append(copy)
+    share = src[late_kind].shape[0] // n
+
+    def own(origin):
+        rows = pl.ds(origin * share, share)
+        return pltpu.make_async_copy(src[late_kind].at[rows], dst[late_kind].at[rows], sem.at[sum(parts)])
+
     for copy in copies:
         copy.start()
+
+    @pl.when(~bottom & ~top)
+    def _():
+        for copy in kept:
+            copy.start()
+        for copy in kept:
+            copy.wait()
+
+    for flag, origin in ((bottom, 0), (top, n - 1)):
+
+        @pl.when(flag)
+        def _():
+            own(origin).start()
+            own(origin).wait()
+
     for copy in copies:
         copy.wait()
 
 
-def place(arrays):
+def place(n, units, arrays):
     parts = [2 if x.shape[0] % 128 == 0 else 1 for x in arrays]
+    vmem, hbm = pl.BlockSpec(memory_space=pltpu.VMEM), pl.BlockSpec(memory_space=pltpu.HBM)
     return pl.pallas_call(
-        functools.partial(put, parts),
-        out_shape=[jax.ShapeDtypeStruct(x.shape, x.dtype) for x in arrays],
-        in_specs=[pl.BlockSpec(memory_space=pltpu.VMEM)] * len(arrays),
-        out_specs=[pl.BlockSpec(memory_space=pltpu.HBM)] * len(arrays),
-        scratch_shapes=[pltpu.SemaphoreType.DMA((sum(parts),))],
+        functools.partial(put, n, units, parts),
+        out_shape=[pltpu.HBM(x.shape, x.dtype) for x in arrays] + [pltpu.VMEM((8, 128), jnp.float32)],
+        in_specs=[vmem] * len(arrays),
+        out_specs=[hbm] * len(arrays) + [vmem],
+        scratch_shapes=[pltpu.SemaphoreType.DMA((sum(parts) + 1,))],
         compiler_params=pltpu.CompilerParams(vmem_limit_bytes=24 * 1024 * 1024),
         name="place",
     )(*arrays)
 
 
-def shards(n, tps, *args):
+def last_hop(n, units, have, after, got, send_sem, recv_sem):
+    z, late = lax.axis_index("rows"), lax.axis_index("unit") == units - 1
+    bottom, top = ends(n, units)
+    size = got.shape[0]
+    share = have.shape[0] - size
+
+    def hop(direction):
+        return pltpu.make_async_remote_copy(
+            src_ref=have.at[pl.ds(share * direction, size)],
+            dst_ref=got,
+            send_sem=send_sem.at[direction],
+            recv_sem=recv_sem.at[direction],
+            device_id={"rows": z + 1 - 2 * direction},
+            device_id_type=MESH,
+        )
+
+    barrier = pltpu.get_barrier_semaphore()
+    above, below = late & (z == n - 2), late & (z == 1)
+
+    @pl.when(bottom)
+    def _():
+        pl.semaphore_signal(barrier, inc=1, device_id={"rows": z + 1}, device_id_type=MESH)
+
+    @pl.when(top)
+    def _():
+        pl.semaphore_signal(barrier, inc=1, device_id={"rows": z - 1}, device_id_type=MESH)
+
+    @pl.when(above | below)
+    def _():
+        pl.semaphore_wait(barrier, above.astype(jnp.int32) + below.astype(jnp.int32))
+
+    for direction, flag in ((0, above), (1, below)):
+
+        @pl.when(flag)
+        def _():
+            hop(direction).start()
+
+    for direction, flag in ((0, top), (1, bottom)):
+
+        @pl.when(flag)
+        def _():
+            hop(direction).wait_recv()
+
+    for direction, flag in ((0, above), (1, below)):
+
+        @pl.when(flag)
+        def _():
+            hop(direction).wait_send()
+
+
+def finish(n, units, have, after):
+    share = have.shape[0] // n
+    vmem, dma = pl.BlockSpec(memory_space=pltpu.VMEM), pltpu.SemaphoreType.DMA
+    return pl.pallas_call(
+        functools.partial(last_hop, n, units),
+        out_shape=pltpu.VMEM((have.shape[0] - share, have.shape[1]), have.dtype),
+        in_specs=[vmem, vmem],
+        out_specs=vmem,
+        scratch_shapes=[dma((2,)), dma((2,))],
+        compiler_params=pltpu.CompilerParams(
+            collective_id=1, has_side_effects=True, vmem_limit_bytes=4 * 1024 * 1024
+        ),
+        name="last_hop",
+    )(have, after)
+
+
+def add_rows(n, units, got, old, out, sem):
+    size = got.shape[0]
+    share = out.shape[0] - size
+    for flag, start in zip(ends(n, units), (share, 0)):
+
+        @pl.when(flag)
+        def _():
+            copy = pltpu.make_async_copy(got, out.at[pl.ds(start, size)], sem)
+            copy.start()
+            copy.wait()
+
+
+def complete(n, units, got, old):
+    vmem, hbm = pl.BlockSpec(memory_space=pltpu.VMEM), pl.BlockSpec(memory_space=pltpu.HBM)
+    return pl.pallas_call(
+        functools.partial(add_rows, n, units),
+        out_shape=pltpu.HBM(old.shape, old.dtype),
+        in_specs=[vmem, hbm],
+        out_specs=hbm,
+        scratch_shapes=[pltpu.SemaphoreType.DMA],
+        input_output_aliases={1: 0},
+        compiler_params=pltpu.CompilerParams(vmem_limit_bytes=4 * 1024 * 1024),
+        name="complete",
+    )(got, old)
+
+
+def shards(n, tps, units, *args):
     w, low, high = args[0:12:3], [x.T for x in args[1:12:3]], args[2:12:3]
     norm_train, norm_step = args[12].reshape(1, -1), args[13].reshape(1, -1)
     kinds = len(w)
     by_column = [False] * (kinds - 1) + [True]
     stacked = [by_column[k] and w[k].shape[1] % 128 != 0 for k in range(kinds)]
-    most = {order[0]: first_bytes, order[1]: chunk_bytes}
-    pieces = [pieces_of(*w[k].shape, most.get(k, w[k].size * 2)) for k in range(kinds)]
-    count = sum(pieces)
+    firsts = {order[0]: (64, 128), order[1]: (160,)}
+    pieces = [pieces_of(w[k].shape[0], firsts.get(k, ())) for k in range(kinds)]
+    count = sum(map(len, pieces))
     shapes = []
     for k in range(kinds):
         rows, columns = w[k].shape
@@ -332,7 +482,7 @@
     dma = pltpu.SemaphoreType.DMA
     operands = (*w, *low, *high, norm_train, norm_step)
     results = pl.pallas_call(
-        functools.partial(kernel, n, tps, stacked, pieces),
+        functools.partial(kernel, n, tps, units, stacked, pieces),
         out_shape=[pltpu.VMEM(s, jnp.bfloat16) for s in shapes]
         + [pltpu.VMEM((total // width, width), jnp.bfloat16)],
         in_specs=[hbm] * (3 * kinds + 2),
@@ -351,15 +501,18 @@
             dma((2, n, kinds)),
             dma((2, n)),
             dma((2, n)),
-            dma((tps,)),
-            dma((tps,)),
+            dma((tps, tps)),
+            dma((tps, tps)),
         ],
         compiler_params=pltpu.CompilerParams(
             collective_id=0, has_side_effects=True, vmem_limit_bytes=24 * 1024 * 1024
         ),
         name="merge_and_gather",
     )(*[pltpu.with_memory_space_constraint(x, pltpu.HBM) for x in operands])
-    results = place(results)
+    have = results[late_kind]
+    *results, after = place(n, units, results)
+    if n > 1:
+        results[late_kind] = complete(n, units, finish(n, units, have, after), results[late_kind])
     finals = []
     for k in range(kinds):
         full = results[k]
@@ -371,7 +524,7 @@
 
 def solution(mesh):
     return jax.shard_map(
-        functools.partial(shards, mesh.shape["rows"], mesh.shape["tp"]),
+        functools.partial(shards, mesh.shape["rows"], mesh.shape["tp"], mesh.shape["unit"]),
         mesh=mesh,
         in_specs=(
             P(("unit", "rows"), "tp"),

time: 224 us -> 218 us (0.973)
  Pallas kernels: 221 us -> 217 us
    pallas_call x2 -> x4, Pallas kernels: 221 us -> 217 us  [the longest x1 198 us: shards(): pl.pallas_call(functools.partial(kernel, n, tps, units, stacked, pieces),...]
where the time goes in v1:
time: 218 us; the launch traced here: 217 us
  Pallas kernels  217 us (100%)
    pallas_call x1, Pallas kernels, shards(): pl.pallas_call(functools.partial(kernel, n, tps, units, stacked, pieces),...  198 us
    pallas_call x1, Pallas kernels, finish(): pl.pallas_call(functools.partial(last_hop, n, units), out_shape=pltpu.VME...  13 us
    pallas_call x1, Pallas kernels, place(): pl.pallas_call(functools.partial(put, n, units, parts), out_shape=[pltpu....  4.53 us

profile of v1, /device:TPU:1, one launch (start us, length us, event | category | flops | bytes accessed | tf_op | source)
XLA Modules:
  0.0 217.5 jit_solution(9996160509258058866)
XLA Ops:
  0.6 198.3 %merge_and_gather.1 = (bf16[2560,1024]{1,0:T(8,128)(2,1)S(1)}, bf16[2560,256]{1,0:T(8,128)(2,1)S(1)}, bf16[2560,256]{1,0:T(8,128)(2,1)S(1)}, bf16[1024,2560]{1,0:T(8,128)(2,1)S(1)}, bf16[20,128]{1,0:T(8,128)(2,1)S(1)}) custom-call(bf16[640,1024]{1,0:T(8,128)(2,1)} %refs_0_.1, bf16[640,256]{1,0:T(8,128)(2,1)} %refs_1_.1, bf16[640,256]{1,0:T(8,128)(2,1)} %refs_2_.1, ...), custom_call_target="tpu_custom_call" | custom-call | tf_op jit(solution)/shard_map/merge_and_gather/pallas_call | solution.py:484
  199.0 4.5 %place.1 = (bf16[2560,1024]{1,0:T(8,128)(2,1)}, bf16[2560,256]{1,0:T(8,128)(2,1)}, bf16[2560,256]{1,0:T(8,128)(2,1)}, bf16[1024,2560]{1,0:T(8,128)(2,1)}, bf16[20,128]{1,0:T(8,128)(2,1)}, /*index=5*/f32[8,128]{1,0:T(8,128)S(1)}) custom-call(bf16[2560,1024]{1,0:T(8,128)(2,1)S(1)} %get-tuple-element.16.refs_0_, ...), custom_call_target="tpu_custom_call" | custom-call | tf_op jit(solution)/shard_map/place/pallas_call | solution.py:357
  203.5 13.0 %last_hop.1.got = bf16[1920,256]{1,0:T(8,128)(2,1)S(1)} custom-call(bf16[2560,256]{1,0:T(8,128)(2,1)S(1)} %get-tuple-element.18.refs_2_.have, f32[8,128]{1,0:T(8,128)S(1)} %get-tuple-element.23.after), custom_call_target="tpu_custom_call" | custom-call | tf_op jit(solution)/shard_map/last_hop/pallas_call | solution.py:421
  216.5 1.0 complete.1

commit v2 on v1

--- a/solution.py
+++ b/solution.py
@@ -90,8 +90,6 @@
             if k == kind:
                 load(i).start()
 
-    load_kind(order[0])
-
     barrier = pltpu.get_barrier_semaphore()
 
     @pl.when(has_up)
@@ -105,7 +103,7 @@
     for partner in [exchange[0] for exchanges in rounds for exchange in exchanges]:
         pl.semaphore_signal(barrier, inc=1, device_id={"tp": partner}, device_id_type=MESH)
 
-    for kind in order[1:]:
+    for kind in order:
         load_kind(kind)
 
     norm_loads = [
@@ -142,17 +140,17 @@
     def whole_hop(k, origin, direction):
         return hop(
             region(k, None, origin),
-            pass_send.at[direction, origin, k],
-            pass_recv.at[direction, origin, k],
+            pass_send.at[origin, k],
+            pass_recv.at[origin, k],
             direction,
         )
 
-    def norm_hop(origin, direction):
+    def norm_hop(origin, direction, own=0):
         return pltpu.make_async_remote_copy(
             src_ref=norm_all.at[origin, t],
             dst_ref=norm_all.at[origin, t],
-            send_sem=norm_send.at[direction, origin],
-            recv_sem=norm_recv.at[direction, origin],
+            send_sem=norm_send.at[own * direction, origin],
+            recv_sem=norm_recv.at[origin],
             device_id={"rows": z + 1 - 2 * direction},
             device_id_type=MESH,
         )
@@ -214,7 +212,8 @@
         if p == 0:
             for copy in side(k):
                 copy.wait()
-            low_rows[k][...] = low_own[k][...].astype(jnp.float32).T.astype(jnp.bfloat16)
+        mine = pl.ds(*rows_of(k, p))
+        low_rows[k][mine, :] = low_own[k][:, mine].astype(jnp.float32).T.astype(jnp.bfloat16)
         load(i).wait()
         merge(i)
         if i == 1:
@@ -227,7 +226,7 @@
                 copy.wait()
             norm_all[z, t] = (norm_own[0] + norm_own[1]).astype(jnp.bfloat16).astype(jnp.float32)
         if i == min(4, len(chunks) - 1):
-            send_both(functools.partial(norm_hop, z))
+            send_both(functools.partial(norm_hop, z, own=1))
     send_both(functools.partial(chunk_hop, len(chunks) - 1, z), chunks[-1][0])
 
     def arrival(arrived, onward, d, k=None):
@@ -244,30 +243,33 @@
 
     def distance(d, _, near=False):
         arrival([norm_hop], norm_hop, d)
-
-        @pl.when(d == n - 1)
-        def _():
-            cross_start(0)
-
         for j, k in enumerate(order):
+
+            @pl.when(d == n - 1)
+            def _():
+                norm_round(j)
+
             onward = functools.partial(whole_hop, k)
             arrived = [onward]
             if near:
                 arrived = [functools.partial(chunk_hop, i) for i, c in enumerate(chunks) if c[0] == k]
-            if k == order[-1]:
-
-                @pl.when(d == n - 1)
-                def _():
-                    all_norms()
-
             arrival(arrived, onward, d, k)
         return 0
 
-    def all_norms():
-        for r in range(len(rounds)):
-            if r > 0:
-                cross_start(r)
-            cross_wait(r)
+    def norm_round(j):
+        last = len(rounds)
+        if 0 < j <= last:
+            cross_wait(j - 1)
+        if j < last:
+            cross_start(j)
+        if j == min(last, kinds - 1):
+            for r in range(j, last):
+                cross_wait(r)
+                if r + 1 < last:
+                    cross_start(r + 1)
+            write_norm()
+
+    def write_norm():
         line = jnp.concatenate([norm_all[a, b] for a in range(n) for b in range(tps)], axis=1)
         width = norm_out.shape[1]
         norm_out[...] = jnp.concatenate(
@@ -286,7 +288,7 @@
 
         @pl.when(sends(None, direction))
         def _():
-            norm_hop(z, direction).wait_send()
+            norm_hop(z, direction, own=1).wait_send()
 
     def drain(origin, _):
         for direction, passed in ((0, origin < z), (1, origin > z)):
@@ -463,9 +465,11 @@
     kinds = len(w)
     by_column = [False] * (kinds - 1) + [True]
     stacked = [by_column[k] and w[k].shape[1] % 128 != 0 for k in range(kinds)]
-    firsts = {order[0]: (64, 128), order[1]: (160,)}
+    firsts = {order[0]: (128, 128), order[1]: (128,)}
     pieces = [pieces_of(w[k].shape[0], firsts.get(k, ())) for k in range(kinds)]
     count = sum(map(len, pieces))
+    rounds = rounds_of(tps, 0)
+    crossings = (len(rounds), max(map(len, rounds), default=0))
     shapes = []
     for k in range(kinds):
         rows, columns = w[k].shape
@@ -497,12 +501,12 @@
             dma((2, kinds)),
             dma((2, count)),
             dma((2, count)),
-            dma((2, n, kinds)),
-            dma((2, n, kinds)),
+            dma((n, kinds)),
+            dma((n, kinds)),
             dma((2, n)),
-            dma((2, n)),
-            dma((tps, tps)),
-            dma((tps, tps)),
+            dma((n,)),
+            dma(crossings),
+            dma(crossings),
         ],
         compiler_params=pltpu.CompilerParams(
             collective_id=0, has_side_effects=True, vmem_limit_bytes=24 * 1024 * 1024

time: 218 us -> 217 us (level)
    pallas_call x1, Pallas kernels: 198 us -> 194 us  [shards(): pl.pallas_call(functools.partial(kernel, n, tps, units, stacked, pieces),...]
    pallas_call x1, Pallas kernels: 13 us -> 16.5 us  [finish(): pl.pallas_call(functools.partial(last_hop, n, units), out_shape=pltpu.VME...]
where the time goes in v2:
time: 217 us
  Pallas kernels  216 us (100%)
    pallas_call x1, Pallas kernels, shards(): pl.pallas_call(functools.partial(kernel, n, tps, units, stacked, pieces),...  194 us
    pallas_call x1, Pallas kernels, finish(): pl.pallas_call(functools.partial(last_hop, n, units), out_shape=pltpu.VME...  16.5 us
    pallas_call x1, Pallas kernels, place(): pl.pallas_call(functools.partial(put, n, units, parts), out_shape=[pltpu....  4.53 us

profile of v2, /device:TPU:1, one launch (start us, length us, event | category | flops | bytes accessed | tf_op | source)
XLA Modules:
  0.0 216.8 jit_solution(6082831149878956612)
XLA Ops:
  0.6 194.1 %merge_and_gather.1 = (bf16[2560,1024]{1,0:T(8,128)(2,1)S(1)}, bf16[2560,256]{1,0:T(8,128)(2,1)S(1)}, bf16[2560,256]{1,0:T(8,128)(2,1)S(1)}, bf16[1024,2560]{1,0:T(8,128)(2,1)S(1)}, bf16[20,128]{1,0:T(8,128)(2,1)S(1)}) custom-call(bf16[640,1024]{1,0:T(8,128)(2,1)} %refs_0_.1, bf16[640,256]{1,0:T(8,128)(2,1)} %refs_1_.1, bf16[640,256]{1,0:T(8,128)(2,1)} %refs_2_.1, ...), custom_call_target="tpu_custom_call" | custom-call | tf_op jit(solution)/shard_map/merge_and_gather/pallas_call | solution.py:488
  194.8 4.5 %place.1 = (bf16[2560,1024]{1,0:T(8,128)(2,1)}, bf16[2560,256]{1,0:T(8,128)(2,1)}, bf16[2560,256]{1,0:T(8,128)(2,1)}, bf16[1024,2560]{1,0:T(8,128)(2,1)}, bf16[20,128]{1,0:T(8,128)(2,1)}, /*index=5*/f32[8,128]{1,0:T(8,128)S(1)}) custom-call(bf16[2560,1024]{1,0:T(8,128)(2,1)S(1)} %get-tuple-element.16.refs_0_, ...), custom_call_target="tpu_custom_call" | custom-call | tf_op jit(solution)/shard_map/place/pallas_call | solution.py:359
  199.3 16.5 %last_hop.1.got = bf16[1920,256]{1,0:T(8,128)(2,1)S(1)} custom-call(bf16[2560,256]{1,0:T(8,128)(2,1)S(1)} %get-tuple-element.18.refs_2_.have, f32[8,128]{1,0:T(8,128)S(1)} %get-tuple-element.23.after), custom_call_target="tpu_custom_call" | custom-call | tf_op jit(solution)/shard_map/last_hop/pallas_call | solution.py:423
  215.8 1.0 complete.1

commit v3 on v2

--- a/solution.py
+++ b/solution.py
@@ -49,13 +49,16 @@
     w_own, low_own, high_own = refs[:kinds], refs[kinds : 2 * kinds], refs[2 * kinds : 3 * kinds]
     low_rows = refs[3 * kinds : 4 * kinds]
     refs = refs[4 * kinds :]
-    norm_own, norm_all, norm_sem, load_sem, side_sem, send_sem, recv_sem, pass_send, pass_recv, norm_send, norm_recv, cross_send, cross_recv = refs
+    norm_own, norm_all, norm_sem, load_sem, side_sem, send_sem, recv_sem, pass_send, pass_recv, norm_send, norm_recv, down_sem, cross_send, cross_recv = refs
 
     z, t = lax.axis_index("rows"), lax.axis_index("tp")
     late = lax.axis_index("unit") == units - 1
     rounds = rounds_of(tps, t)
     chunks = [(k, p) for k in order for p in range(len(pieces[k]))]
     has_up, has_down = z < n - 1, z > 0
+    middle, top = n // 2, z == n - 1
+    greeted = (has_up & (z >= middle), has_down & (z <= middle))
+    waits = (has_up & ~greeted[0], has_down & ~greeted[1])
     held_up, held_down = late & (z == n - 2), late & (z == 1)
     missing_up, missing_down = late & (z == n - 1), late & (z == 0)
 
@@ -92,16 +95,18 @@
 
     barrier = pltpu.get_barrier_semaphore()
 
-    @pl.when(has_up)
+    @pl.when(z < middle)
     def _():
         pl.semaphore_signal(barrier, inc=1, device_id={"rows": z + 1}, device_id_type=MESH)
 
-    @pl.when(has_down)
+    @pl.when(z > middle)
     def _():
         pl.semaphore_signal(barrier, inc=1, device_id={"rows": z - 1}, device_id_type=MESH)
 
-    for partner in [exchange[0] for exchanges in rounds for exchange in exchanges]:
-        pl.semaphore_signal(barrier, inc=1, device_id={"tp": partner}, device_id_type=MESH)
+    @pl.when(top)
+    def _():
+        for partner in [exchange[0] for exchanges in rounds for exchange in exchanges]:
+            pl.semaphore_signal(barrier, inc=1, device_id={"tp": partner}, device_id_type=MESH)
 
     for kind in order:
         load_kind(kind)
@@ -145,13 +150,23 @@
             direction,
         )
 
-    def norm_hop(origin, direction, own=0):
+    def norm_hop(origin):
         return pltpu.make_async_remote_copy(
             src_ref=norm_all.at[origin, t],
             dst_ref=norm_all.at[origin, t],
-            send_sem=norm_send.at[own * direction, origin],
+            send_sem=norm_send.at[origin],
             recv_sem=norm_recv.at[origin],
-            device_id={"rows": z + 1 - 2 * direction},
+            device_id={"rows": z + 1},
+            device_id_type=MESH,
+        )
+
+    def norm_down():
+        return pltpu.make_async_remote_copy(
+            src_ref=norm_out,
+            dst_ref=norm_out,
+            send_sem=down_sem.at[0],
+            recv_sem=down_sem.at[1],
+            device_id={"rows": z - 1},
             device_id_type=MESH,
         )
 
@@ -175,12 +190,26 @@
         for j in range(len(rounds[r])):
             cross(r, j, coming=True).wait_recv()
 
-    def send_both(make, k=None):
+    def send_greeted(i):
         for direction in range(2):
 
-            @pl.when(sends(k, direction))
-            def _():
-                make(direction).start()
+            @pl.when(sends(chunks[i][0], direction) & greeted[direction])
+            def _():
+                chunk_hop(i, z, direction).start()
+
+    def send_late():
+        for direction in range(2):
+
+            @pl.when(waits[direction])
+            def _():
+                chunk_hop(0, z + 1 - 2 * direction, 1 - direction).wait_recv()
+                if direction == 0:
+                    norm_hop(z).start()
+                for i, (k, _) in enumerate(chunks):
+
+                    @pl.when(sends(k, direction))
+                    def _():
+                        chunk_hop(i, z, direction).start()
 
     def merge(i):
         k, p = chunks[i]
@@ -214,60 +243,80 @@
                 copy.wait()
         mine = pl.ds(*rows_of(k, p))
         low_rows[k][mine, :] = low_own[k][:, mine].astype(jnp.float32).T.astype(jnp.bfloat16)
+        if i == 1:
+            partners = greeted[0].astype(jnp.int32) + greeted[1].astype(jnp.int32)
+            partners += top.astype(jnp.int32) * sum(map(len, rounds))
+
+            @pl.when(partners > 0)
+            def _():
+                pl.semaphore_wait(barrier, partners)
+
+        if i > 0:
+            send_greeted(i - 1)
         load(i).wait()
         merge(i)
-        if i == 1:
-            partners = has_up.astype(jnp.int32) + has_down.astype(jnp.int32) + sum(map(len, rounds))
-            pl.semaphore_wait(barrier, partners)
-        if i > 0:
-            send_both(functools.partial(chunk_hop, i - 1, z), chunks[i - 1][0])
         if i == min(3, len(chunks) - 2):
             for copy in norm_loads:
                 copy.wait()
             norm_all[z, t] = (norm_own[0] + norm_own[1]).astype(jnp.bfloat16).astype(jnp.float32)
         if i == min(4, len(chunks) - 1):
-            send_both(functools.partial(norm_hop, z, own=1))
-    send_both(functools.partial(chunk_hop, len(chunks) - 1, z), chunks[-1][0])
-
-    def arrival(arrived, onward, d, k=None):
+
+            @pl.when(greeted[0])
+            def _():
+                norm_hop(z).start()
+
+    send_greeted(len(chunks) - 1)
+    send_late()
+
+    def arrival(arrived, onward, d, k, near):
         for direction, origin in ((0, z - d), (1, z + d)):
 
             @pl.when(comes(k, d, direction))
             def _():
-                for make in arrived:
-                    make(origin, direction).wait_recv()
+                for j, make in enumerate(arrived):
+                    if near and k == order[0] and j == 0:
+
+                        @pl.when(~waits[1 - direction])
+                        def _():
+                            make(origin, direction).wait_recv()
+
+                    else:
+                        make(origin, direction).wait_recv()
 
                 @pl.when(sends(k, direction))
                 def _():
                     onward(origin, direction).start()
 
     def distance(d, _, near=False):
-        arrival([norm_hop], norm_hop, d)
+        @pl.when(z - d >= 0)
+        def _():
+            norm_hop(z - d).wait_recv()
+
+            @pl.when(has_up)
+            def _():
+                norm_hop(z - d).start()
+
         for j, k in enumerate(order):
 
-            @pl.when(d == n - 1)
-            def _():
-                norm_round(j)
+            @pl.when(top & (d == n - 1))
+            def _():
+                if j == 0:
+                    share_norm()
+                if j == 1:
+                    norm_down().start()
 
             onward = functools.partial(whole_hop, k)
             arrived = [onward]
             if near:
                 arrived = [functools.partial(chunk_hop, i) for i, c in enumerate(chunks) if c[0] == k]
-            arrival(arrived, onward, d, k)
+            arrival(arrived, onward, d, k, near)
         return 0
 
-    def norm_round(j):
-        last = len(rounds)
-        if 0 < j <= last:
-            cross_wait(j - 1)
-        if j < last:
-            cross_start(j)
-        if j == min(last, kinds - 1):
-            for r in range(j, last):
-                cross_wait(r)
-                if r + 1 < last:
-                    cross_start(r + 1)
-            write_norm()
+    def share_norm():
+        for r in range(len(rounds)):
+            cross_start(r)
+            cross_wait(r)
+        write_norm()
 
     def write_norm():
         line = jnp.concatenate([norm_all[a, b] for a in range(n) for b in range(tps)], axis=1)
@@ -279,6 +328,14 @@
     distance(jnp.int32(1), 0, near=True)
     lax.fori_loop(2, n, distance, 0)
 
+    @pl.when(has_up)
+    def _():
+        norm_down().wait_recv()
+
+    @pl.when(has_up & has_down)
+    def _():
+        norm_down().start()
+
     for direction in range(2):
         for i in range(len(chunks)):
 
@@ -286,9 +343,13 @@
             def _():
                 chunk_hop(i, z, direction).wait_send()
 
-        @pl.when(sends(None, direction))
-        def _():
-            norm_hop(z, direction, own=1).wait_send()
+    @pl.when(has_up)
+    def _():
+        norm_hop(z).wait_send()
+
+    @pl.when(has_down)
+    def _():
+        norm_down().wait_send()
 
     def drain(origin, _):
         for direction, passed in ((0, origin < z), (1, origin > z)):
@@ -298,16 +359,19 @@
                 def _():
                     whole_hop(k, origin, direction).wait_send()
 
-            @pl.when(sends(None, direction) & passed)
-            def _():
-                norm_hop(origin, direction).wait_send()
+        @pl.when(has_up & (origin < z))
+        def _():
+            norm_hop(origin).wait_send()
 
         return 0
 
     lax.fori_loop(0, n, drain, 0)
-    for r in range(len(rounds)):
-        for j in range(len(rounds[r])):
-            cross(r, j).wait_send()
+
+    @pl.when(top)
+    def _():
+        for r in range(len(rounds)):
+            for j in range(len(rounds[r])):
+                cross(r, j).wait_send()
 
 
 def ends(n, units):
@@ -503,8 +567,9 @@
             dma((2, count)),
             dma((n, kinds)),
             dma((n, kinds)),
-            dma((2, n)),
             dma((n,)),
+            dma((n,)),
+            dma((2,)),
             dma(crossings),
             dma(crossings),
         ],

time: 217 us -> 217 us (level)
  no operation moved by 1% of the time
where the time goes in v3:
time: 217 us
  Pallas kernels  216 us (100%)
    pallas_call x1, Pallas kernels, shards(): pl.pallas_call(functools.partial(kernel, n, tps, units, stacked, pieces),...  194 us
    pallas_call x1, Pallas kernels, finish(): pl.pallas_call(functools.partial(last_hop, n, units), out_shape=pltpu.VME...  16.3 us
    pallas_call x1, Pallas kernels, place(): pl.pallas_call(functools.partial(put, n, units, parts), out_shape=[pltpu....  4.53 us

profile of v3, /device:TPU:1, one launch (start us, length us, event | category | flops | bytes accessed | tf_op | source)
XLA Modules:
  0.0 216.7 jit_solution(9195256115190869229)
XLA Ops:
  0.6 194.3 %merge_and_gather.1 = (bf16[2560,1024]{1,0:T(8,128)(2,1)S(1)}, bf16[2560,256]{1,0:T(8,128)(2,1)S(1)}, bf16[2560,256]{1,0:T(8,128)(2,1)S(1)}, bf16[1024,2560]{1,0:T(8,128)(2,1)S(1)}, bf16[20,128]{1,0:T(8,128)(2,1)S(1)}) custom-call(bf16[640,1024]{1,0:T(8,128)(2,1)} %refs_0_.1, bf16[640,256]{1,0:T(8,128)(2,1)} %refs_1_.1, bf16[640,256]{1,0:T(8,128)(2,1)} %refs_2_.1, ...), custom_call_target="tpu_custom_call" | custom-call | tf_op jit(solution)/shard_map/merge_and_gather/pallas_call | solution.py:552
  194.9 4.5 %place.1 = (bf16[2560,1024]{1,0:T(8,128)(2,1)}, bf16[2560,256]{1,0:T(8,128)(2,1)}, bf16[2560,256]{1,0:T(8,128)(2,1)}, bf16[1024,2560]{1,0:T(8,128)(2,1)}, bf16[20,128]{1,0:T(8,128)(2,1)}, /*index=5*/f32[8,128]{1,0:T(8,128)S(1)}) custom-call(bf16[2560,1024]{1,0:T(8,128)(2,1)S(1)} %get-tuple-element.16.refs_0_, ...), custom_call_target="tpu_custom_call" | custom-call | tf_op jit(solution)/shard_map/place/pallas_call | solution.py:423
  199.4 16.3 %last_hop.1.got = bf16[1920,256]{1,0:T(8,128)(2,1)S(1)} custom-call(bf16[2560,256]{1,0:T(8,128)(2,1)S(1)} %get-tuple-element.18.refs_2_.have, f32[8,128]{1,0:T(8,128)S(1)} %get-tuple-element.23.after), custom_call_target="tpu_custom_call" | custom-call | tf_op jit(solution)/shard_map/last_hop/pallas_call | solution.py:487
  215.7 1.0 complete.1

commit v4 on v3

--- a/solution.py
+++ b/solution.py
@@ -243,6 +243,8 @@
                 copy.wait()
         mine = pl.ds(*rows_of(k, p))
         low_rows[k][mine, :] = low_own[k][:, mine].astype(jnp.float32).T.astype(jnp.bfloat16)
+        load(i).wait()
+        merge(i)
         if i == 1:
             partners = greeted[0].astype(jnp.int32) + greeted[1].astype(jnp.int32)
             partners += top.astype(jnp.int32) * sum(map(len, rounds))
@@ -253,8 +255,6 @@
 
         if i > 0:
             send_greeted(i - 1)
-        load(i).wait()
-        merge(i)
         if i == min(3, len(chunks) - 2):
             for copy in norm_loads:
                 copy.wait()
@@ -529,7 +529,7 @@
     kinds = len(w)
     by_column = [False] * (kinds - 1) + [True]
     stacked = [by_column[k] and w[k].shape[1] % 128 != 0 for k in range(kinds)]
-    firsts = {order[0]: (128, 128), order[1]: (128,)}
+    firsts = {order[0]: (128, 128), order[1]: (256,)}
     pieces = [pieces_of(w[k].shape[0], firsts.get(k, ())) for k in range(kinds)]
     count = sum(map(len, pieces))
     rounds = rounds_of(tps, 0)

time: 217 us -> 217 us (level)
  no operation moved by 1% of the time
where the time goes in v4:
time: 217 us
  Pallas kernels  216 us (100%)
    pallas_call x1, Pallas kernels, shards(): pl.pallas_call(functools.partial(kernel, n, tps, units, stacked, pieces),...  194 us
    pallas_call x1, Pallas kernels, finish(): pl.pallas_call(functools.partial(last_hop, n, units), out_shape=pltpu.VME...  16.3 us
    pallas_call x1, Pallas kernels, place(): pl.pallas_call(functools.partial(put, n, units, parts), out_shape=[pltpu....  4.53 us

profile of v4, /device:TPU:1, one launch (start us, length us, event | category | flops | bytes accessed | tf_op | source)
XLA Modules:
  0.0 216.9 jit_solution(1694529590025392304)
XLA Ops:
  0.6 194.4 %merge_and_gather.1 = (bf16[2560,1024]{1,0:T(8,128)(2,1)S(1)}, bf16[2560,256]{1,0:T(8,128)(2,1)S(1)}, bf16[2560,256]{1,0:T(8,128)(2,1)S(1)}, bf16[1024,2560]{1,0:T(8,128)(2,1)S(1)}, bf16[20,128]{1,0:T(8,128)(2,1)S(1)}) custom-call(bf16[640,1024]{1,0:T(8,128)(2,1)} %refs_0_.1, bf16[640,256]{1,0:T(8,128)(2,1)} %refs_1_.1, bf16[640,256]{1,0:T(8,128)(2,1)} %refs_2_.1, ...), custom_call_target="tpu_custom_call" | custom-call | tf_op jit(solution)/shard_map/merge_and_gather/pallas_call | solution.py:552
  195.1 4.5 %place.1 = (bf16[2560,1024]{1,0:T(8,128)(2,1)}, bf16[2560,256]{1,0:T(8,128)(2,1)}, bf16[2560,256]{1,0:T(8,128)(2,1)}, bf16[1024,2560]{1,0:T(8,128)(2,1)}, bf16[20,128]{1,0:T(8,128)(2,1)}, /*index=5*/f32[8,128]{1,0:T(8,128)S(1)}) custom-call(bf16[2560,1024]{1,0:T(8,128)(2,1)S(1)} %get-tuple-element.16.refs_0_, ...), custom_call_target="tpu_custom_call" | custom-call | tf_op jit(solution)/shard_map/place/pallas_call | solution.py:423
  199.6 16.3 %last_hop.1.got = bf16[1920,256]{1,0:T(8,128)(2,1)S(1)} custom-call(bf16[2560,256]{1,0:T(8,128)(2,1)S(1)} %get-tuple-element.18.refs_2_.have, f32[8,128]{1,0:T(8,128)S(1)} %get-tuple-element.23.after), custom_call_target="tpu_custom_call" | custom-call | tf_op jit(solution)/shard_map/last_hop/pallas_call | solution.py:487
  215.9 1.0 complete.1

commit v5 on v3

--- a/solution.py
+++ b/solution.py
@@ -529,7 +529,7 @@
     kinds = len(w)
     by_column = [False] * (kinds - 1) + [True]
     stacked = [by_column[k] and w[k].shape[1] % 128 != 0 for k in range(kinds)]
-    firsts = {order[0]: (128, 128), order[1]: (128,)}
+    firsts = {order[0]: (128, 128), order[1]: ()}
     pieces = [pieces_of(w[k].shape[0], firsts.get(k, ())) for k in range(kinds)]
     count = sum(map(len, pieces))
     rounds = rounds_of(tps, 0)

time: 217 us -> 217 us (level)
  no operation moved by 1% of the time
where the time goes in v5:
time: 217 us
  Pallas kernels  216 us (100%)
    pallas_call x1, Pallas kernels, shards(): pl.pallas_call(functools.partial(kernel, n, tps, units, stacked, pieces),...  194 us
    pallas_call x1, Pallas kernels, finish(): pl.pallas_call(functools.partial(last_hop, n, units), out_shape=pltpu.VME...  16.3 us
    pallas_call x1, Pallas kernels, place(): pl.pallas_call(functools.partial(put, n, units, parts), out_shape=[pltpu....  4.53 us

profile of v5, /device:TPU:1, one launch (start us, length us, event | category | flops | bytes accessed | tf_op | source)
XLA Modules:
  0.0 216.7 jit_solution(16390142013967743493)
XLA Ops:
  0.6 194.2 %merge_and_gather.1 = (bf16[2560,1024]{1,0:T(8,128)(2,1)S(1)}, bf16[2560,256]{1,0:T(8,128)(2,1)S(1)}, bf16[2560,256]{1,0:T(8,128)(2,1)S(1)}, bf16[1024,2560]{1,0:T(8,128)(2,1)S(1)}, bf16[20,128]{1,0:T(8,128)(2,1)S(1)}) custom-call(bf16[640,1024]{1,0:T(8,128)(2,1)} %refs_0_.1, bf16[640,256]{1,0:T(8,128)(2,1)} %refs_1_.1, bf16[640,256]{1,0:T(8,128)(2,1)} %refs_2_.1, ...), custom_call_target="tpu_custom_call" | custom-call | tf_op jit(solution)/shard_map/merge_and_gather/pallas_call | solution.py:552
  194.9 4.5 %place.1 = (bf16[2560,1024]{1,0:T(8,128)(2,1)}, bf16[2560,256]{1,0:T(8,128)(2,1)}, bf16[2560,256]{1,0:T(8,128)(2,1)}, bf16[1024,2560]{1,0:T(8,128)(2,1)}, bf16[20,128]{1,0:T(8,128)(2,1)}, /*index=5*/f32[8,128]{1,0:T(8,128)S(1)}) custom-call(bf16[2560,1024]{1,0:T(8,128)(2,1)S(1)} %get-tuple-element.16.refs_0_, ...), custom_call_target="tpu_custom_call" | custom-call | tf_op jit(solution)/shard_map/place/pallas_call | solution.py:423
  199.4 16.3 %last_hop.1.got = bf16[1920,256]{1,0:T(8,128)(2,1)S(1)} custom-call(bf16[2560,256]{1,0:T(8,128)(2,1)S(1)} %get-tuple-element.18.refs_2_.have, f32[8,128]{1,0:T(8,128)S(1)} %get-tuple-element.23.after), custom_call_target="tpu_custom_call" | custom-call | tf_op jit(solution)/shard_map/last_hop/pallas_call | solution.py:487
  215.7 1.0 complete.1

commit v6 on v5

--- a/solution.py
+++ b/solution.py
@@ -437,15 +437,18 @@
     size = got.shape[0]
     share = have.shape[0] - size
 
-    def hop(direction):
-        return pltpu.make_async_remote_copy(
-            src_ref=have.at[pl.ds(share * direction, size)],
-            dst_ref=got,
-            send_sem=send_sem.at[direction],
-            recv_sem=recv_sem.at[direction],
-            device_id={"rows": z + 1 - 2 * direction},
-            device_id_type=MESH,
-        )
+    def hops(direction):
+        return [
+            pltpu.make_async_remote_copy(
+                src_ref=have.at[pl.ds(share * (direction + j), share)],
+                dst_ref=got.at[pl.ds(share * j, share)],
+                send_sem=send_sem.at[direction, j],
+                recv_sem=recv_sem.at[direction, j],
+                device_id={"rows": z + 1 - 2 * direction},
+                device_id_type=MESH,
+            )
+            for j in range(n - 1)
+        ]
 
     barrier = pltpu.get_barrier_semaphore()
     above, below = late & (z == n - 2), late & (z == 1)
@@ -466,19 +469,22 @@
 
         @pl.when(flag)
         def _():
-            hop(direction).start()
+            for hop in hops(direction):
+                hop.start()
 
     for direction, flag in ((0, top), (1, bottom)):
 
         @pl.when(flag)
         def _():
-            hop(direction).wait_recv()
+            for hop in hops(direction):
+                hop.wait_recv()
 
     for direction, flag in ((0, above), (1, below)):
 
         @pl.when(flag)
         def _():
-            hop(direction).wait_send()
+            for hop in hops(direction):
+                hop.wait_send()
 
 
 def finish(n, units, have, after):
@@ -489,7 +495,7 @@
         out_shape=pltpu.VMEM((have.shape[0] - share, have.shape[1]), have.dtype),
         in_specs=[vmem, vmem],
         out_specs=vmem,
-        scratch_shapes=[dma((2,)), dma((2,))],
+        scratch_shapes=[dma((2, n - 1)), dma((2, n - 1))],
         compiler_params=pltpu.CompilerParams(
             collective_id=1, has_side_effects=True, vmem_limit_bytes=4 * 1024 * 1024
         ),

time: 217 us -> 217 us (level)
  no operation moved by 1% of the time
where the time goes in v6:
time: 217 us
  Pallas kernels  216 us (100%)
    pallas_call x1, Pallas kernels, shards(): pl.pallas_call(functools.partial(kernel, n, tps, units, stacked, pieces),...  194 us
    pallas_call x1, Pallas kernels, finish(): pl.pallas_call(functools.partial(last_hop, n, units), out_shape=pltpu.VME...  16.4 us
    pallas_call x1, Pallas kernels, place(): pl.pallas_call(functools.partial(put, n, units, parts), out_shape=[pltpu....  4.53 us

profile of v6, /device:TPU:1, one launch (start us, length us, event | category | flops | bytes accessed | tf_op | source)
XLA Modules:
  0.0 216.8 jit_solution(3962624354275094444)
XLA Ops:
  0.6 194.2 %merge_and_gather.1 = (bf16[2560,1024]{1,0:T(8,128)(2,1)S(1)}, bf16[2560,256]{1,0:T(8,128)(2,1)S(1)}, bf16[2560,256]{1,0:T(8,128)(2,1)S(1)}, bf16[1024,2560]{1,0:T(8,128)(2,1)S(1)}, bf16[20,128]{1,0:T(8,128)(2,1)S(1)}) custom-call(bf16[640,1024]{1,0:T(8,128)(2,1)} %refs_0_.1, bf16[640,256]{1,0:T(8,128)(2,1)} %refs_1_.1, bf16[640,256]{1,0:T(8,128)(2,1)} %refs_2_.1, ...), custom_call_target="tpu_custom_call" | custom-call | tf_op jit(solution)/shard_map/merge_and_gather/pallas_call | solution.py:558
  194.9 4.5 %place.1 = (bf16[2560,1024]{1,0:T(8,128)(2,1)}, bf16[2560,256]{1,0:T(8,128)(2,1)}, bf16[2560,256]{1,0:T(8,128)(2,1)}, bf16[1024,2560]{1,0:T(8,128)(2,1)}, bf16[20,128]{1,0:T(8,128)(2,1)}, /*index=5*/f32[8,128]{1,0:T(8,128)S(1)}) custom-call(bf16[2560,1024]{1,0:T(8,128)(2,1)S(1)} %get-tuple-element.16.refs_0_, ...), custom_call_target="tpu_custom_call" | custom-call | tf_op jit(solution)/shard_map/place/pallas_call | solution.py:423
  199.4 16.4 %last_hop.1.got = bf16[1920,256]{1,0:T(8,128)(2,1)S(1)} custom-call(bf16[2560,256]{1,0:T(8,128)(2,1)S(1)} %get-tuple-element.18.refs_2_.have, f32[8,128]{1,0:T(8,128)S(1)} %get-tuple-element.23.after), custom_call_target="tpu_custom_call" | custom-call | tf_op jit(solution)/shard_map/last_hop/pallas_call | solution.py:493
  215.8 1.0 complete.1

commit v7 on v6

--- a/solution.py
+++ b/solution.py
@@ -510,9 +510,16 @@
 
         @pl.when(flag)
         def _():
-            copy = pltpu.make_async_copy(got, out.at[pl.ds(start, size)], sem)
-            copy.start()
-            copy.wait()
+            copies = [
+                pltpu.make_async_copy(
+                    got.at[pl.ds(j * share, share)], out.at[pl.ds(start + j * share, share)], sem.at[j]
+                )
+                for j in range(n - 1)
+            ]
+            for copy in copies:
+                copy.start()
+            for copy in copies:
+                copy.wait()
 
 
 def complete(n, units, got, old):
@@ -522,7 +529,7 @@
         out_shape=pltpu.HBM(old.shape, old.dtype),
         in_specs=[vmem, hbm],
         out_specs=hbm,
-        scratch_shapes=[pltpu.SemaphoreType.DMA],
+        scratch_shapes=[pltpu.SemaphoreType.DMA((n - 1,))],
         input_output_aliases={1: 0},
         compiler_params=pltpu.CompilerParams(vmem_limit_bytes=4 * 1024 * 1024),
         name="complete",

time: 217 us -> 217 us (level)
  no operation moved by 1% of the time
where the time goes in v7:
time: 217 us
  Pallas kernels  216 us (100%)
    pallas_call x1, Pallas kernels, shards(): pl.pallas_call(functools.partial(kernel, n, tps, units, stacked, pieces),...  194 us
    pallas_call x1, Pallas kernels, finish(): pl.pallas_call(functools.partial(last_hop, n, units), out_shape=pltpu.VME...  16.4 us
    pallas_call x1, Pallas kernels, place(): pl.pallas_call(functools.partial(put, n, units, parts), out_shape=[pltpu....  4.53 us

profile of v7, /device:TPU:1, one launch (start us, length us, event | category | flops | bytes accessed | tf_op | source)
XLA Modules:
  0.0 216.8 jit_solution(7883704312195117750)
XLA Ops:
  0.6 194.2 %merge_and_gather.1 = (bf16[2560,1024]{1,0:T(8,128)(2,1)S(1)}, bf16[2560,256]{1,0:T(8,128)(2,1)S(1)}, bf16[2560,256]{1,0:T(8,128)(2,1)S(1)}, bf16[1024,2560]{1,0:T(8,128)(2,1)S(1)}, bf16[20,128]{1,0:T(8,128)(2,1)S(1)}) custom-call(bf16[640,1024]{1,0:T(8,128)(2,1)} %refs_0_.1, bf16[640,256]{1,0:T(8,128)(2,1)} %refs_1_.1, bf16[640,256]{1,0:T(8,128)(2,1)} %refs_2_.1, ...), custom_call_target="tpu_custom_call" | custom-call | tf_op jit(solution)/shard_map/merge_and_gather/pallas_call | solution.py:565
  194.9 4.5 %place.1 = (bf16[2560,1024]{1,0:T(8,128)(2,1)}, bf16[2560,256]{1,0:T(8,128)(2,1)}, bf16[2560,256]{1,0:T(8,128)(2,1)}, bf16[1024,2560]{1,0:T(8,128)(2,1)}, bf16[20,128]{1,0:T(8,128)(2,1)}, /*index=5*/f32[8,128]{1,0:T(8,128)S(1)}) custom-call(bf16[2560,1024]{1,0:T(8,128)(2,1)S(1)} %get-tuple-element.16.refs_0_, ...), custom_call_target="tpu_custom_call" | custom-call | tf_op jit(solution)/shard_map/place/pallas_call | solution.py:423
  199.4 16.4 %last_hop.1.got = bf16[1920,256]{1,0:T(8,128)(2,1)S(1)} custom-call(bf16[2560,256]{1,0:T(8,128)(2,1)S(1)} %get-tuple-element.18.refs_2_.have, f32[8,128]{1,0:T(8,128)S(1)} %get-tuple-element.23.after), custom_call_target="tpu_custom_call" | custom-call | tf_op jit(solution)/shard_map/last_hop/pallas_call | solution.py:493
  215.8 1.0 complete.1
